TPU v7x, 256 devices: a whole 4x4x8 slice. The times are simulated.
256 devices in a mesh: lat: 32 (over y_hi, z, core), lon: 8 (over y_lo, x).
Axes of the slice: x: 4, y: 4 (y_hi: 2, y_lo: 2; y = y_hi * 2 + y_lo), z: 8, core: 2. Of those that a mesh axis runs over, the one named last changes fastest.
Arguments:
- field: bfloat16 [384, 768, 512], P('lat', 'lon'), may hold values from -6 to 6
- quad_weight: float32 [384], P('lat'), may hold values from 0.5 to 1.5
- legendre: bfloat16 [384, 384, 384], P('lat'), as said below
- filter_real: float32 [384, 512], replicated, may hold values from -4 to 4
- filter_imag: float32 [384, 512], replicated, may hold values from -4 to 4
- neighbour: int32 [384, 12], P('lat'), may hold values from 0 to 24
- basis: int32 [384, 12], P('lat'), may hold values from 0 to 7
- disco_quad: float32 [384, 12], P('lat'), may hold values from 0.5 to 1.5
- disco_weight: float32 [8, 512], replicated, may hold values from -2 to 2
- norm_gain: float32 [512], replicated, may hold values from 0.5 to 1.5
- w_in: bfloat16 [512, 1024], replicated, may hold values from -0.25 to 0.25
- b_in: float32 [1024], replicated, may hold values from -3 to 3
- w_out: bfloat16 [1024, 512], replicated, may hold values from -0.1875 to 0.1875
- b_out: float32 [512], replicated, may hold values from -3 to 3
Outputs:
- block_out: bfloat16 [384, 768, 512], P('lat', 'lon')
- spatial: bfloat16 [384, 768, 512], P('lat', 'lon')
Inputs may be any that keep to these rules, and one draw needn't show every extreme that they name: legendre[m, l, t] = 0 for l < m.
All inputs are finite; a program needn't handle non-finite values.
Results may differ from a plain program's by a relative error of at most 0.018.
Values may be sent and summed in bfloat16 or wider, within the bound.
A program may use at most 64 MiB of HBM per device.

v0:
```python
import math
import jax
import jax.numpy as jnp
from jax import lax
from jax.sharding import PartitionSpec as P

HALO = 2
KB = 8
NWIN = 25
exact_mode = lax.Precision.HIGHEST


def padded_2(block, sides, width):
    for axis, dim in sides:
        count = lax.axis_size(axis)
        forward = [(i, i + 1) for i in range(count - 1)]
        backward = [(target, source) for source, target in forward]
        low = lax.ppermute(
            lax.slice_in_dim(block, block.shape[dim] - width, None, axis=dim), axis, forward
        )
        high = lax.ppermute(lax.slice_in_dim(block, 0, width, axis=dim), axis, backward)
        block = jnp.concatenate([low, block, high], axis=dim)
    return block


def split_table(table):
    upper = table.astype(jnp.bfloat16)
    lower = (table - upper.astype(jnp.float32)).astype(jnp.bfloat16)
    return (upper, lower)


def fourier_tables(nlon, mmax):
    points = jnp.arange(nlon, dtype=jnp.int32)
    waves = jnp.arange(mmax, dtype=jnp.int32)
    phase = waves[:, None] * points[None, :] % nlon
    angle = phase.astype(jnp.float32) * (2.0 * math.pi / nlon)
    cosine = jnp.cos(angle) / math.sqrt(nlon)
    sine = jnp.sin(angle) / math.sqrt(nlon)
    forward_table = jnp.stack([cosine, -sine], axis=0)
    factor = jnp.where(waves == 0, 1.0, 2.0).astype(jnp.float32)[:, None]
    inverse_table = jnp.stack([factor * cosine, -factor * sine], axis=0)
    return (forward_table, inverse_table)


def window_kernel(neighbour, basis, disco_quad, weight_cols):
    places = (neighbour[:, :, None] == jnp.arange(NWIN, dtype=jnp.int32)[None, None, :]).astype(
        jnp.float32
    )
    places = places * disco_quad[:, :, None]
    kinds = (basis[:, :, None] == jnp.arange(KB, dtype=jnp.int32)[None, None, :]).astype(
        jnp.float32
    )
    mixing = jnp.einsum("isn,isb->inb", places, kinds, precision=exact_mode)
    return jnp.einsum("inb,bc->inc", mixing, weight_cols, precision=exact_mode)


def convolve(padded, kernel, lat_rows, lon_cols):
    span = 2 * HALO + 1
    total = jnp.zeros((lat_rows, lon_cols, kernel.shape[2]), jnp.float32)
    for offset in range(NWIN):
        row_shift = offset // span
        col_shift = offset % span
        window = padded[row_shift : row_shift + lat_rows, col_shift : col_shift + lon_cols, :]
        total = total + kernel[:, offset, None, :] * window
    return total


def channel_mlp(spatial, field, norm_gain, w_in, b_in, w_out, b_out):
    channels = spatial.shape[-1]
    tokens = spatial.reshape(-1, channels).astype(jnp.float32)
    center = jnp.mean(tokens, axis=1, keepdims=True)
    spread = jnp.mean((tokens - center) ** 2, axis=1, keepdims=True)
    normed = ((tokens - center) * lax.rsqrt(spread + 1e-05) * norm_gain).astype(jnp.bfloat16)
    hidden = jnp.dot(normed, w_in, preferred_element_type=jnp.float32) + b_in
    hidden = jax.nn.gelu(hidden).astype(jnp.bfloat16)
    result = jnp.dot(hidden, w_out, preferred_element_type=jnp.float32)
    result = result + b_out + field.reshape(-1, channels).astype(jnp.float32)
    return result.astype(jnp.bfloat16).reshape(field.shape)


def shards(
    field,
    quad_weight,
    legendre,
    filter_real,
    filter_imag,
    neighbour,
    basis,
    disco_quad,
    disco_weight,
    norm_gain,
    w_in,
    b_in,
    w_out,
    b_out,
):
    lat_rows, lon_cols, channels = field.shape
    lon_count = lax.axis_size("lon")
    lat_count = lax.axis_size("lat")
    nlon = lon_cols * lon_count
    wave_block = legendre.shape[0]
    mmax = wave_block * lat_count
    cblock = channels // lon_count
    forward_table, inverse_table = fourier_tables(nlon, mmax)
    forward_upper, forward_lower = split_table(forward_table)
    inverse_upper, inverse_lower = split_table(inverse_table)
    columns = lax.all_to_all(field, "lon", split_axis=2, concat_axis=1, tiled=True)
    frequency = jnp.einsum(
        "tkc,rmk->rmtc", columns, forward_upper, preferred_element_type=jnp.float32
    )
    frequency = frequency + jnp.einsum(
        "tkc,rmk->rmtc", columns, forward_lower, preferred_element_type=jnp.float32
    )
    weighted = (frequency * quad_weight[None, None, :, None]).astype(jnp.bfloat16)
    weighted = jnp.transpose(weighted, (1, 2, 0, 3))
    coeffs = jnp.einsum(
        "mlt,mtrc->mlrc",
        legendre,
        lax.all_to_all(weighted, "lat", split_axis=0, concat_axis=1, tiled=True),
        preferred_element_type=jnp.float32,
    )
    chan_start = lax.axis_index("lon") * cblock
    gain_real = lax.dynamic_slice_in_dim(filter_real, chan_start, cblock, 1)[None, :, :]
    gain_imag = lax.dynamic_slice_in_dim(filter_imag, chan_start, cblock, 1)[None, :, :]
    real_part = coeffs[:, :, 0]
    imag_part = coeffs[:, :, 1]
    filtered = jnp.stack(
        [
            gain_real * real_part - gain_imag * imag_part,
            gain_real * imag_part + gain_imag * real_part,
        ],
        axis=2,
    ).astype(jnp.bfloat16)
    synthesis = jnp.einsum(
        "mlt,mlrc->mtrc", legendre, filtered, preferred_element_type=jnp.float32
    ).astype(jnp.bfloat16)
    lat_block = lax.all_to_all(synthesis, "lat", split_axis=1, concat_axis=0, tiled=True)
    wave = jnp.einsum("mtrc,rmk->tkc", lat_block, inverse_upper, preferred_element_type=jnp.float32)
    wave = wave + jnp.einsum(
        "mtrc,rmk->tkc", lat_block, inverse_lower, preferred_element_type=jnp.float32
    )
    wave = wave.astype(jnp.bfloat16)
    weight_cols = lax.dynamic_slice_in_dim(disco_weight, chan_start, cblock, 1)
    kernel = window_kernel(neighbour, basis, disco_quad, weight_cols)
    cycle = jnp.concatenate([wave[:, nlon - HALO :], wave, wave[:, :HALO]], axis=1)
    padded = padded_2(cycle, (("lat", 0),), HALO)
    conv = convolve(padded, kernel, lat_rows, nlon)
    spatial_part = (wave.astype(jnp.float32) + conv).astype(jnp.bfloat16)
    spatial = lax.all_to_all(spatial_part, "lon", split_axis=1, concat_axis=2, tiled=True)
    block_out = channel_mlp(spatial, field, norm_gain, w_in, b_in, w_out, b_out)
    return (block_out, spatial)


def solution(mesh):
    placed = (
        P("lat", "lon", None),
        P("lat"),
        P("lat", None, None),
        P(),
        P(),
        P("lat", None),
        P("lat", None),
        P("lat", None),
        P(),
        P(),
        P(),
        P(),
        P(),
        P(),
    )
    return jax.shard_map(
        shards,
        mesh=mesh,
        in_specs=placed,
        out_specs=(P("lat", "lon", None), P("lat", "lon", None)),
        check_vma=False,
    )
```

profile of v0, /device:TPU:16, one launch (start us, length us, event | category | flops | bytes accessed | tf_op | source)
XLA Modules:
  0.0 266.1 jit_solution(6598086077392066688)
XLA Ops:
  0.6 4.5 %copy.55 = bf16[12,96,512]{1,0,2:T(8,128)(2,1)} copy(bf16[12,96,512]{2,1,0:T(8,128)(2,1)} %param.14) | data formatting | bytes 2359296 | tf_op args[0]
  5.1 5.0 %all-to-all-start = ((bf16[12,96,512]{1,0,2:T(8,128)(2,1)}), bf16[12,96,512]{1,0,2:T(8,128)(2,1)}, u32[]{:S(2)}, u32[]{:S(2)}) async-start(bf16[12,96,512]{1,0,2:T(8,128)(2,1)} %copy.55), calls=%async_computation | async-start | bytes 4194304 | tf_op jit(solution)/shard_map/all_to_all | solution.py:107
  10.2 6.4 %multiply_negate_fusion = (f32[1,384,768]{2,1,0:T(8,128)}, f32[1,384,768]{2,1,0:T(8,128)}) fusion(), kind=kLoop, calls=%fused_computation.79 | loop fusion | flops 3538944 | bytes 2359296 | tf_op jit(solution)/shard_map/neg | solution.py:39
  16.5 20.7 %all-to-all-done = bf16[12,96,512]{1,0,2:T(8,128)(2,1)} async-done(((bf16[12,96,512]{1,0,2:T(8,128)(2,1)}), bf16[12,96,512]{1,0,2:T(8,128)(2,1)}, u32[]{:S(2)}, u32[]{:S(2)}) %all-to-all-start) | async-done | bytes 1179680 | tf_op jit(solution)/shard_map/all_to_all | solution.py:107
  37.2 3.8 %copy.57 = bf16[12,8,96,64]{2,1,3,0:T(8,128)(2,1)} copy(bf16[12,8,96,64]{2,0,3,1:T(8,128)(2,1)} %bitcast.4) | data formatting | bytes 2359296 | tf_op jit(solution)/shard_map/all_to_all | solution.py:107
  41.0 3.8 %reshape.182 = bf16[12,768,64,1]{1,2,0,3:T(8,128)(2,1)} reshape(bf16[12,8,96,64]{2,1,3,0:T(8,128)(2,1)} %copy.57) | data formatting | bytes 2359296 | tf_op jit(solution)/shard_map/all_to_all | solution.py:107
  50.3 6.7 %copy.58 = bf16[384,12,2,64]{3,2,1,0:T(2,128)(2,1)} copy(bf16[384,12,2,64]{0,3,1,2:T(8,128)(2,1)} %fusion.41) | data formatting | bytes 2359296 | tf_op jit(solution)/shard_map/convert_element_type | solution.py:114
  56.9 6.3 %reshape.191 = bf16[32,2,9216]{2,1,0:T(2,128)(2,1)} reshape(bf16[384,12,2,64]{3,2,1,0:T(2,128)(2,1)} %copy.58) | data formatting | bytes 2359296
  63.2 11.8 %all-to-all-start.1 = ((bf16[32,2,9216]{2,1,0:T(2,128)(2,1)}), bf16[32,2,9216]{2,1,0:T(2,128)(2,1)}, u32[]{:S(2)}, u32[]{:S(2)}) async-start(bf16[32,2,9216]{2,1,0:T(2,128)(2,1)} %reshape.191), calls=%async_computation.1 | async-start | bytes 2359296 | tf_op jit(solution)/shard_map/all_to_all | solution.py:119
  86.9 17.9 %all-to-all-done.1 = bf16[32,2,9216]{2,1,0:T(2,128)(2,1)} async-done(((bf16[32,2,9216]{2,1,0:T(2,128)(2,1)}), bf16[32,2,9216]{2,1,0:T(2,128)(2,1)}, u32[]{:S(2)}, u32[]{:S(2)}) %all-to-all-start.1) | async-done | bytes 1179680 | tf_op jit(solution)/shard_map/all_to_all | solution.py:119
  104.8 6.3 %reshape.192 = bf16[384,12,2,64]{3,2,1,0:T(2,128)(2,1)} reshape(bf16[32,2,9216]{2,1,0:T(2,128)(2,1)} %all-to-all-done.1) | data formatting | bytes 2359296
  118.8 5.6 %copy.62 = bf16[12,384,2,64]{3,2,0,1:T(2,128)(2,1)S(1)} copy(bf16[12,384,2,64]{1,3,2,0:T(8,128)(2,1)} %fusion.43) | data formatting | bytes 2359296 | tf_op jit(solution)/shard_map/convert_element_type | solution.py:136
  126.7 7.1 %all-to-all-start.2 = ((bf16[32,2,9216]{2,1,0:T(2,128)(2,1)}), bf16[32,2,9216]{2,1,0:T(2,128)(2,1)S(1)}, u32[]{:S(2)}, u32[]{:S(2)}) async-start(bf16[32,2,9216]{2,1,0:T(2,128)(2,1)} %reshape.193), calls=%async_computation.2 | async-start | bytes 2359296 | tf_op jit(solution)/shard_map/all_to_all | solution.py:137
  140.8 6.0 %fusion.71 = (f32[1,384,768]{2,1,0:T(8,128)}, f32[1,384,768]{2,1,0:T(8,128)}) fusion(f32[384]{0:T(512)S(1)} %copy-done.46, f32[384]{0:T(512)S(1)} %copy-done.47), kind=kLoop, calls=%fused_computation.86 | loop fusion | flops 3244032 | bytes 2362368 | tf_op jit(solution)/shard_map/mul | solution.py:41
  146.8 16.7 %all-to-all-done.2 = bf16[32,2,9216]{2,1,0:T(2,128)(2,1)S(1)} async-done(((bf16[32,2,9216]{2,1,0:T(2,128)(2,1)}), bf16[32,2,9216]{2,1,0:T(2,128)(2,1)S(1)}, u32[]{:S(2)}, u32[]{:S(2)}) %all-to-all-start.2) | async-done | bytes 1179680 | tf_op jit(solution)/shard_map/all_to_all | solution.py:137
  167.9 5.9 %copy.65 = bf16[384,12,2,64]{0,3,2,1:T(8,128)(2,1)S(1)} copy(bf16[384,12,2,64]{3,2,1,0:T(2,128)(2,1)} %bitcast.151) | data formatting | bytes 2359296 | tf_op jit(solution)/shard_map/all_to_all | solution.py:137
  178.6 7.3 %collective-permute-start.1 = (bf16[2,772,64]{1,2,0:T(8,128)(2,1)S(1)}, bf16[2,772,64]{1,2,0:T(8,128)(2,1)S(1)}, u32[]{:S(2)}, u32[]{:S(2)}) collective-permute-start(bf16[2,772,64]{1,2,0:T(8,128)(2,1)S(1)} %get-tuple-element.13), channel_id=1, source_target_pairs={{8,0},{16,8},{24,16},{32,24},{40,32},{48,40},{56,48},{64,56},{72,6... | collective-permute-start | bytes 592904 | tf_op jit(solution)/shard_map/ppermute | solution.py:21
  191.6 15.5 %fusion.29 = bf16[12,768,64]{1,2,0:T(8,128)(2,1)} fusion(bf16[12,768,64]{1,2,0:T(8,128)(2,1)S(1)} %fusion.42, bf16[12,2,64]{1,2,0:T(8,128)(2,1)S(1)} %get-tuple-element.15, bf16[12,2,64]{1,2,0:T(8,128)(2,1)S(1)} %get-tuple-element.14, bf16[14,772,64]{1,2,0:T(8,128)(2,1)S(1)} %get-tuple-element.11, bf16[14,772,64]{1,2,0:T(8,128)(2,1)S(1)} %get-tuple-element.10, ...), kind=kLoop, calls=%fused_computation.42 | loop fusion | flops 51904512 | bytes 26035200 | tf_op jit(solution)/shard_map/convert_element_type | solution.py:148
  207.1 3.9 %copy.67 = bf16[12,768,64]{2,0,1:T(8,128)(2,1)S(1)} copy(bf16[12,768,64]{1,2,0:T(8,128)(2,1)} %fusion.29) | data formatting | bytes 2359296 | tf_op jit(solution)/shard_map/convert_element_type | solution.py:148
  213.9 22.6 %all_to_all.72 = bf16[8,2,36864]{2,1,0:T(2,128)(2,1)S(1)} all-to-all(bf16[8,2,36864]{2,1,0:T(2,128)(2,1)} %reshape.195), channel_id=1, replica_groups=mesh['lat'=32,'lon'=8] {'lon'}, dimensions={0} | all-to-all | bytes 2359296 | tf_op jit(solution)/shard_map/all_to_all | solution.py:149
  239.7 3.9 %copy.68 = bf16[12,8,96,64]{2,3,1,0:T(8,128)(2,1)S(1)} copy(bf16[12,8,96,64]{3,0,2,1:T(8,128)(2,1)} %bitcast.146) | data formatting | bytes 2359296 | tf_op jit(solution)/shard_map/all_to_all | solution.py:149
  246.5 5.7 %copy.69 = f32[12,96,8,64]{1,0,3,2:T(8,128)} copy(f32[12,96,8,64]{1,3,2,0:T(8,128)} %bitcast_convert_fusion) | data formatting | bytes 4718592 | tf_op jit(solution)/shard_map/convert_element_type | solution.py:70
  252.2 5.1 %reshape.179 = f32[1152,512]{0,1:T(8,128)} reshape(f32[12,96,8,64]{1,0,3,2:T(8,128)} %copy.69) | data formatting | bytes 4718592 | tf_op jit(solution)/shard_map/convert_element_type | solution.py:70
  258.9 7.2 %fusion.13 = bf16[1152,512]{1,0:T(8,128)(2,1)} fusion(bf16[1024,512]{1,0:T(8,128)(2,1)} %param.26, bf16[1152,512]{1,0:T(8,128)(2,1)} %bitcast.153, f32[512]{0:T(512)} %param.27, bf16[512,1024]{1,0:T(8,128)(2,1)} %param.24, f32[1024]{0:T(1024)} %param.25, f32[1152,512]{0,1:T(8,128)} %reshape.179, f32[512]{0:T(512)} %param.23, f32[1152]{0:T(1024)S(1)} %rsqrt.12, ...), kind=kOutput, calls=%fused_computation.17 | convolution fusion | flops 2432434176 | bytes 6833152 | tf_op jit(solution)/shard_map/dot_general | solution.py:76
  (151 shorter events, 59.3 us)
Async XLA Ops:
  0.6 114.1 %copy-start = (bf16[12,384,384]{2,1,0:T(8,128)(2,1)S(1)}, bf16[12,384,384]{2,1,0:T(8,128)(2,1)}, u32[]{:S(2)}) copy-start(bf16[12,384,384]{2,1,0:T(8,128)(2,1)} %param.16) | copy-start | bytes 10616836
  5.1 32.1 %all-to-all-start = ((bf16[12,96,512]{1,0,2:T(8,128)(2,1)}), bf16[12,96,512]{1,0,2:T(8,128)(2,1)}, u32[]{:S(2)}, u32[]{:S(2)}) async-start(bf16[12,96,512]{1,0,2:T(8,128)(2,1)} %copy.55), calls=%async_computation | async-start | bytes 4194304 | tf_op jit(solution)/shard_map/all_to_all | solution.py:107
  63.2 17.1 %copy-start.48 = (f32[12,12]{1,0:T(8,128)S(1)}, f32[12,12]{1,0:T(8,128)}, u32[]{:S(2)}) copy-start(f32[12,12]{1,0:T(8,128)} %param.21) | copy-start | bytes 1732
  63.2 17.1 %copy-start.49 = (s32[12,12]{1,0:T(8,128)S(1)}, s32[12,12]{1,0:T(8,128)}, u32[]{:S(2)}) copy-start(s32[12,12]{1,0:T(8,128)} %param.19) | copy-start | bytes 1732
  63.2 41.6 %all-to-all-start.1 = ((bf16[32,2,9216]{2,1,0:T(2,128)(2,1)}), bf16[32,2,9216]{2,1,0:T(2,128)(2,1)}, u32[]{:S(2)}, u32[]{:S(2)}) async-start(bf16[32,2,9216]{2,1,0:T(2,128)(2,1)} %reshape.191), calls=%async_computation.1 | async-start | bytes 2359296 | tf_op jit(solution)/shard_map/all_to_all | solution.py:119
  126.6 7.3 %copy-start.44 = (f32[12,1,64]{2,1,0:T(1,128)S(1)}, f32[12,1,64]{2,1,0:T(1,128)}, u32[]{:S(2)}) copy-start(f32[12,1,64]{2,1,0:T(1,128)} %get-tuple-element.23) | copy-start | bytes 9220
  126.6 7.3 %copy-start.45 = (f32[12,1,64]{2,1,0:T(1,128)S(1)}, f32[12,1,64]{2,1,0:T(1,128)}, u32[]{:S(2)}) copy-start(f32[12,1,64]{2,1,0:T(1,128)} %get-tuple-element.24) | copy-start | bytes 9220
  126.6 7.9 %copy-start.42 = (f32[12,1,64]{2,1,0:T(1,128)S(1)}, f32[12,1,64]{2,1,0:T(1,128)}, u32[]{:S(2)}) copy-start(f32[12,1,64]{2,1,0:T(1,128)} %get-tuple-element.25) | copy-start | bytes 9220
  126.6 7.9 %copy-start.43 = (f32[12,1,64]{2,1,0:T(1,128)S(1)}, f32[12,1,64]{2,1,0:T(1,128)}, u32[]{:S(2)}) copy-start(f32[12,1,64]{2,1,0:T(1,128)} %get-tuple-element.26) | copy-start | bytes 9220
  126.6 8.5 %copy-start.40 = (f32[12,1,64]{2,1,0:T(1,128)S(1)}, f32[12,1,64]{2,1,0:T(1,128)}, u32[]{:S(2)}) copy-start(f32[12,1,64]{2,1,0:T(1,128)} %get-tuple-element.27) | copy-start | bytes 9220
  126.6 8.5 %copy-start.41 = (f32[12,1,64]{2,1,0:T(1,128)S(1)}, f32[12,1,64]{2,1,0:T(1,128)}, u32[]{:S(2)}) copy-start(f32[12,1,64]{2,1,0:T(1,128)} %get-tuple-element.28) | copy-start | bytes 9220
  126.6 9.1 %copy-start.38 = (f32[12,1,64]{2,1,0:T(1,128)S(1)}, f32[12,1,64]{2,1,0:T(1,128)}, u32[]{:S(2)}) copy-start(f32[12,1,64]{2,1,0:T(1,128)} %get-tuple-element.29) | copy-start | bytes 9220
  126.6 9.1 %copy-start.39 = (f32[12,1,64]{2,1,0:T(1,128)S(1)}, f32[12,1,64]{2,1,0:T(1,128)}, u32[]{:S(2)}) copy-start(f32[12,1,64]{2,1,0:T(1,128)} %get-tuple-element.30) | copy-start | bytes 9220
  126.6 9.7 %copy-start.36 = (f32[12,1,64]{2,1,0:T(1,128)S(1)}, f32[12,1,64]{2,1,0:T(1,128)}, u32[]{:S(2)}) copy-start(f32[12,1,64]{2,1,0:T(1,128)} %get-tuple-element.31) | copy-start | bytes 9220
  126.7 9.7 %copy-start.37 = (f32[12,1,64]{2,1,0:T(1,128)S(1)}, f32[12,1,64]{2,1,0:T(1,128)}, u32[]{:S(2)}) copy-start(f32[12,1,64]{2,1,0:T(1,128)} %get-tuple-element.32) | copy-start | bytes 9220
  126.7 10.3 %copy-start.34 = (f32[12,1,64]{2,1,0:T(1,128)S(1)}, f32[12,1,64]{2,1,0:T(1,128)}, u32[]{:S(2)}) copy-start(f32[12,1,64]{2,1,0:T(1,128)} %get-tuple-element.33) | copy-start | bytes 9220
  126.7 10.3 %copy-start.35 = (f32[12,1,64]{2,1,0:T(1,128)S(1)}, f32[12,1,64]{2,1,0:T(1,128)}, u32[]{:S(2)}) copy-start(f32[12,1,64]{2,1,0:T(1,128)} %get-tuple-element.34) | copy-start | bytes 9220
  126.7 14.1 %copy-start.46 = (f32[384]{0:T(512)S(1)}, f32[384]{0:T(512)}, u32[]{:S(2)}) copy-start(f32[384]{0:T(512)} %select_multiply_fusion) | copy-start | bytes 4612
  126.7 14.1 %copy-start.47 = (f32[384]{0:T(512)S(1)}, f32[384]{0:T(512)}, u32[]{:S(2)}) copy-start(f32[384]{0:T(512)} %fusion.83) | copy-start | bytes 4612
  126.7 36.8 %all-to-all-start.2 = ((bf16[32,2,9216]{2,1,0:T(2,128)(2,1)}), bf16[32,2,9216]{2,1,0:T(2,128)(2,1)S(1)}, u32[]{:S(2)}, u32[]{:S(2)}) async-start(bf16[32,2,9216]{2,1,0:T(2,128)(2,1)} %reshape.193), calls=%async_computation.2 | async-start | bytes 2359296 | tf_op jit(solution)/shard_map/all_to_all | solution.py:137
  176.3 9.6 %copy-start.32 = (f32[12,1,64]{2,1,0:T(1,128)S(1)}, f32[12,1,64]{2,1,0:T(1,128)}, u32[]{:S(2)}) copy-start(f32[12,1,64]{2,1,0:T(1,128)} %get-tuple-element.35) | copy-start | bytes 9220
  176.3 9.6 %copy-start.33 = (f32[12,1,64]{2,1,0:T(1,128)S(1)}, f32[12,1,64]{2,1,0:T(1,128)}, u32[]{:S(2)}) copy-start(f32[12,1,64]{2,1,0:T(1,128)} %get-tuple-element.40) | copy-start | bytes 9220
  176.7 11.0 %collective-permute-start = (bf16[2,772,64]{1,2,0:T(8,128)(2,1)S(1)}, bf16[2,772,64]{1,2,0:T(8,128)(2,1)S(1)}, u32[]{:S(2)}, u32[]{:S(2)}) collective-permute-start(bf16[2,772,64]{1,2,0:T(8,128)(2,1)S(1)} %get-tuple-element.12), channel_id=1, source_target_pairs={{0,8},{8,16},{16,24},{24,32},{32,40},{40,48},{48,56},{56,64},{64,7... | collective-permute-start | bytes 592904 | tf_op jit(solution)/shard_map/ppermute | solution.py:18
  178.6 10.8 %collective-permute-start.1 = (bf16[2,772,64]{1,2,0:T(8,128)(2,1)S(1)}, bf16[2,772,64]{1,2,0:T(8,128)(2,1)S(1)}, u32[]{:S(2)}, u32[]{:S(2)}) collective-permute-start(bf16[2,772,64]{1,2,0:T(8,128)(2,1)S(1)} %get-tuple-element.13), channel_id=1, source_target_pairs={{8,0},{16,8},{24,16},{32,24},{40,32},{48,40},{56,48},{64,56},{72,6... | collective-permute-start | bytes 592904 | tf_op jit(solution)/shard_map/ppermute | solution.py:21
  (32 other events, 152.6 us)
where the time goes:
time: 268 us; the launch traced here: 266 us
  local copies, waits for them, and re-layouts  95.1 us (35%)
  waiting for transfers between devices  58.6 us (22%)
  other arithmetic  34.5 us (13%)
  starting transfers between devices  33.1 us (12%)
  blocking collectives  22.6 us (8%)
  matrix products  20.8 us (8%)
    unnamed x123, local copies, waits for them, and re-layouts  35.8 us
    all_to_all x1, blocking collectives, shards(): lax.all_to_all(spatial_part, 'lon', split_axis=1, concat_axis=2, tiled=True)  22.6 us
    all_to_all x1, waiting for transfers between devices, shards(): lax.all_to_all(field, 'lon', split_axis=2, concat_axis=1, tiled=True)  20.7 us
    all_to_all x1, waiting for transfers between devices, shards(): lax.all_to_all(weighted, 'lat', split_axis=0, concat_axis=1, tiled=True)  17.9 us
    all_to_all x1, waiting for transfers between devices, shards(): lax.all_to_all(synthesis, 'lat', split_axis=1, concat_axis=0, tiled=True)  16.7 us
    convert_element_type x1, other arithmetic, shards(): spatial_part = (wave.astype(jnp.float32) + conv).astype(jnp.bfloat16)  15.5 us
    all_to_all x1, starting transfers between devices, shards(): lax.all_to_all(weighted, 'lat', split_axis=0, concat_axis=1, tiled=True)  11.8 us
    convert_element_type x2, local copies, waits for them, and re-layouts, channel_mlp(): tokens = spatial.reshape(-1, channels).astype(jnp.float32)  10.8 us
  transfers between devices with their start and end apart: 5, of which 5 were waited for; matrix products, arithmetic and copies ran while one was open for 11% of the time, Pallas kernels for 0%

commit v1 on v0

--- a/solution.py
+++ b/solution.py
@@ -8,6 +8,11 @@
 KB = 8
 NWIN = 25
 exact_mode = lax.Precision.HIGHEST
+
+
+def cut_tokens_all(field_in):
+    all_values = jnp.stack(jnp.split(field_in, lax.axis_size("lon"), axis=1), axis=0)
+    return jnp.concatenate(lax.all_to_all(all_values, "lon", 0, 0), axis=2)
 
 
 def padded_2(block, sides, width):
@@ -146,7 +151,7 @@
     padded = padded_2(cycle, (("lat", 0),), HALO)
     conv = convolve(padded, kernel, lat_rows, nlon)
     spatial_part = (wave.astype(jnp.float32) + conv).astype(jnp.bfloat16)
-    spatial = lax.all_to_all(spatial_part, "lon", split_axis=1, concat_axis=2, tiled=True)
+    spatial = cut_tokens_all(spatial_part)
     block_out = channel_mlp(spatial, field, norm_gain, w_in, b_in, w_out, b_out)
     return (block_out, spatial)
 

time: 268 us -> 254 us (0.948)
  local copies, waits for them, and re-layouts: 95.1 us -> 80.4 us
  blocking collectives: 22.6 us -> 26.6 us
  other arithmetic: 34.5 us -> 31.6 us
    unnamed x123 -> x128, local copies, waits for them, and re-layouts: 35.8 us -> 30.7 us
    all_to_all x1, blocking collectives: 22.6 us -> 26.6 us  [cut_tokens_all(): return jnp.concatenate(lax.all_to_all(all_values, 'lon', 0, 0), axis=2)]
    convert_element_type x1 -> x0, local copies, waits for them, and re-layouts: 3.92 us -> none  [shards(): spatial_part = (wave.astype(jnp.float32) + conv).astype(jnp.bfloat16)]
    all_to_all x1 -> x0, local copies, waits for them, and re-layouts: 3.87 us -> none  [shards(): lax.all_to_all(spatial_part, 'lon', split_axis=1, concat_axis=2, tiled=True)]
  transfers between devices with their start and end apart: 5 -> 5, of which waited for: 5 -> 5; matrix products, arithmetic and copies ran while one was open for 11% -> 12% of each run, Pallas kernels for 0% -> 0%
where the time goes in v1:
time: 254 us; the launch traced here: 253 us
  local copies, waits for them, and re-layouts  80.4 us (32%)
  waiting for transfers between devices  58.8 us (23%)
  starting transfers between devices  33.1 us (13%)
  other arithmetic  31.6 us (12%)
  blocking collectives  26.6 us (10%)
  matrix products  20.8 us (8%)
    unnamed x128, local copies, waits for them, and re-layouts  30.7 us
    all_to_all x1, blocking collectives, cut_tokens_all(): return jnp.concatenate(lax.all_to_all(all_values, 'lon', 0, 0), axis=2)  26.6 us
    all_to_all x1, waiting for transfers between devices, shards(): lax.all_to_all(field, 'lon', split_axis=2, concat_axis=1, tiled=True)  20.7 us
    all_to_all x1, waiting for transfers between devices, shards(): lax.all_to_all(weighted, 'lat', split_axis=0, concat_axis=1, tiled=True)  17.9 us
    all_to_all x1, waiting for transfers between devices, shards(): lax.all_to_all(synthesis, 'lat', split_axis=1, concat_axis=0, tiled=True)  16.9 us
    convert_element_type x1, other arithmetic, shards(): spatial_part = (wave.astype(jnp.float32) + conv).astype(jnp.bfloat16)  14.3 us
    all_to_all x1, starting transfers between devices, shards(): lax.all_to_all(weighted, 'lat', split_axis=0, concat_axis=1, tiled=True)  11.8 us
    convert_element_type x2, local copies, waits for them, and re-layouts, channel_mlp(): tokens = spatial.reshape(-1, channels).astype(jnp.float32)  8.88 us
  transfers between devices with their start and end apart: 5, of which 5 were waited for; matrix products, arithmetic and copies ran while one was open for 12% of the time, Pallas kernels for 0%

profile of v1, /device:TPU:16, one launch (start us, length us, event | category | flops | bytes accessed | tf_op | source)
XLA Modules:
  0.0 252.8 jit_solution(6298648503651847567)
XLA Ops:
  0.6 4.5 %copy.53 = bf16[12,96,512]{1,0,2:T(8,128)(2,1)} copy(bf16[12,96,512]{2,1,0:T(8,128)(2,1)} %param.14) | data formatting | bytes 2359296 | tf_op args[0]
  5.1 5.0 %all-to-all-start = ((bf16[12,96,512]{1,0,2:T(8,128)(2,1)}), bf16[12,96,512]{1,0,2:T(8,128)(2,1)}, u32[]{:S(2)}, u32[]{:S(2)}) async-start(bf16[12,96,512]{1,0,2:T(8,128)(2,1)} %copy.53), calls=%async_computation | async-start | bytes 4194304 | tf_op jit(solution)/shard_map/all_to_all | solution.py:112
  10.2 6.4 %multiply_negate_fusion = (f32[1,384,768]{2,1,0:T(8,128)}, f32[1,384,768]{2,1,0:T(8,128)}) fusion(), kind=kLoop, calls=%fused_computation.78 | loop fusion | flops 3538944 | bytes 2359296 | tf_op jit(solution)/shard_map/neg | solution.py:44
  16.5 20.7 %all-to-all-done = bf16[12,96,512]{1,0,2:T(8,128)(2,1)} async-done(((bf16[12,96,512]{1,0,2:T(8,128)(2,1)}), bf16[12,96,512]{1,0,2:T(8,128)(2,1)}, u32[]{:S(2)}, u32[]{:S(2)}) %all-to-all-start) | async-done | bytes 1179680 | tf_op jit(solution)/shard_map/all_to_all | solution.py:112
  37.2 3.8 %copy.55 = bf16[12,8,96,64]{2,1,3,0:T(8,128)(2,1)} copy(bf16[12,8,96,64]{2,0,3,1:T(8,128)(2,1)} %bitcast.4) | data formatting | bytes 2359296 | tf_op jit(solution)/shard_map/all_to_all | solution.py:112
  41.0 3.8 %reshape.188 = bf16[12,768,64,1]{1,2,0,3:T(8,128)(2,1)} reshape(bf16[12,8,96,64]{2,1,3,0:T(8,128)(2,1)} %copy.55) | data formatting | bytes 2359296 | tf_op jit(solution)/shard_map/all_to_all | solution.py:112
  44.8 3.2 %fusion.47 = f32[2,384,12,64]{1,3,2,0:T(8,128)S(1)} fusion(bf16[12,768,64,1]{1,2,0,3:T(8,128)(2,1)} %reshape.188, f32[1,384,768]{2,1,0:T(8,128)} %get-tuple-element.41, f32[1,384,768]{2,1,0:T(8,128)} %get-tuple-element.42), kind=kOutput, calls=%fused_computation.60 | convolution fusion | flops 908328960 | bytes 5898240 | tf_op jit(solution)/shard_map/tkc,rmk->rmtc/dot_general | solution.py:113
  50.3 6.7 %copy.56 = bf16[384,12,2,64]{3,2,1,0:T(2,128)(2,1)} copy(bf16[384,12,2,64]{0,3,1,2:T(8,128)(2,1)} %fusion.40) | data formatting | bytes 2359296 | tf_op jit(solution)/shard_map/convert_element_type | solution.py:119
  56.9 6.3 %reshape.197 = bf16[32,2,9216]{2,1,0:T(2,128)(2,1)} reshape(bf16[384,12,2,64]{3,2,1,0:T(2,128)(2,1)} %copy.56) | data formatting | bytes 2359296
  63.2 11.8 %all-to-all-start.1 = ((bf16[32,2,9216]{2,1,0:T(2,128)(2,1)}), bf16[32,2,9216]{2,1,0:T(2,128)(2,1)}, u32[]{:S(2)}, u32[]{:S(2)}) async-start(bf16[32,2,9216]{2,1,0:T(2,128)(2,1)} %reshape.197), calls=%async_computation.1 | async-start | bytes 2359296 | tf_op jit(solution)/shard_map/all_to_all | solution.py:124
  86.9 17.9 %all-to-all-done.1 = bf16[32,2,9216]{2,1,0:T(2,128)(2,1)} async-done(((bf16[32,2,9216]{2,1,0:T(2,128)(2,1)}), bf16[32,2,9216]{2,1,0:T(2,128)(2,1)}, u32[]{:S(2)}, u32[]{:S(2)}) %all-to-all-start.1) | async-done | bytes 1179680 | tf_op jit(solution)/shard_map/all_to_all | solution.py:124
  104.8 6.3 %reshape.198 = bf16[384,12,2,64]{3,2,1,0:T(2,128)(2,1)} reshape(bf16[32,2,9216]{2,1,0:T(2,128)(2,1)} %all-to-all-done.1) | data formatting | bytes 2359296
  111.1 3.7 %copy.57 = bf16[12,32,12,2,64]{4,3,2,1,0:T(2,128)(2,1)S(1)} copy(bf16[12,32,12,2,64]{4,3,2,0,1:T(2,128)(2,1)} %bitcast.172) | data formatting | bytes 2359296 | tf_op jit(solution)/shard_map/all_to_all | solution.py:124
  118.8 5.6 %copy.60 = bf16[12,384,2,64]{3,2,0,1:T(2,128)(2,1)S(1)} copy(bf16[12,384,2,64]{1,3,2,0:T(8,128)(2,1)} %fusion.42) | data formatting | bytes 2359296 | tf_op jit(solution)/shard_map/convert_element_type | solution.py:141
  126.7 7.1 %all-to-all-start.2 = ((bf16[32,2,9216]{2,1,0:T(2,128)(2,1)}), bf16[32,2,9216]{2,1,0:T(2,128)(2,1)S(1)}, u32[]{:S(2)}, u32[]{:S(2)}) async-start(bf16[32,2,9216]{2,1,0:T(2,128)(2,1)} %reshape.199), calls=%async_computation.2 | async-start | bytes 2359296 | tf_op jit(solution)/shard_map/all_to_all | solution.py:142
  140.6 6.0 %fusion.70 = (f32[1,384,768]{2,1,0:T(8,128)}, f32[1,384,768]{2,1,0:T(8,128)}) fusion(f32[384]{0:T(512)S(1)} %copy-done.46, f32[384]{0:T(512)S(1)} %copy-done.47), kind=kLoop, calls=%fused_computation.85 | loop fusion | flops 3244032 | bytes 2362368 | tf_op jit(solution)/shard_map/mul | solution.py:46
  146.6 16.9 %all-to-all-done.2 = bf16[32,2,9216]{2,1,0:T(2,128)(2,1)S(1)} async-done(((bf16[32,2,9216]{2,1,0:T(2,128)(2,1)}), bf16[32,2,9216]{2,1,0:T(2,128)(2,1)S(1)}, u32[]{:S(2)}, u32[]{:S(2)}) %all-to-all-start.2) | async-done | bytes 1179680 | tf_op jit(solution)/shard_map/all_to_all | solution.py:142
  167.9 5.9 %copy.63 = bf16[384,12,2,64]{0,3,2,1:T(8,128)(2,1)S(1)} copy(bf16[384,12,2,64]{3,2,1,0:T(2,128)(2,1)} %bitcast.175) | data formatting | bytes 2359296 | tf_op jit(solution)/shard_map/all_to_all | solution.py:142
  178.6 7.3 %collective-permute-start.1 = (bf16[2,772,64]{1,2,0:T(8,128)(2,1)S(1)}, bf16[2,772,64]{1,2,0:T(8,128)(2,1)S(1)}, u32[]{:S(2)}, u32[]{:S(2)}) collective-permute-start(bf16[2,772,64]{1,2,0:T(8,128)(2,1)S(1)} %get-tuple-element.13), channel_id=1, source_target_pairs={{8,0},{16,8},{24,16},{32,24},{40,32},{48,40},{56,48},{64,56},{72,6... | collective-permute-start | bytes 592904 | tf_op jit(solution)/shard_map/ppermute | solution.py:26
  191.6 14.3 %fusion.29 = bf16[12,768,64]{1,2,0:T(8,128)(2,1)S(1)} fusion(bf16[12,768,64]{1,2,0:T(8,128)(2,1)S(1)} %fusion.41, bf16[12,2,64]{1,2,0:T(8,128)(2,1)S(1)} %get-tuple-element.15, bf16[12,2,64]{1,2,0:T(8,128)(2,1)S(1)} %get-tuple-element.14, bf16[14,772,64]{1,2,0:T(8,128)(2,1)S(1)} %get-tuple-element.11, bf16[14,772,64]{1,2,0:T(8,128)(2,1)S(1)} %get-tuple-element.10, ...), kind=kLoop, calls=%fused_computation.42 | loop fusion | flops 51904512 | bytes 26035200 | tf_op jit(solution)/shard_map/convert_element_type | solution.py:153
  207.0 26.6 %all_to_all.59 = bf16[8,12,96,64]{2,3,1,0:T(8,128)(2,1)S(1)} all-to-all(bf16[8,12,96,64]{2,3,1,0:T(8,128)(2,1)S(1)} %fusion.73), channel_id=1, replica_groups=mesh['lat'=32,'lon'=8] {'lon'}, dimensions={0} | all-to-all | bytes 2359296 | tf_op jit(solution)/shard_map/all_to_all | solution.py:15
  234.0 3.8 %copy.65 = f32[12,96,8,64]{1,0,3,2:T(8,128)} copy(f32[12,96,8,64]{1,3,0,2:T(8,128)S(1)} %bitcast_convert_fusion) | data formatting | bytes 4718592 | tf_op jit(solution)/shard_map/convert_element_type | solution.py:75
  237.8 5.1 %reshape.185 = f32[1152,512]{0,1:T(8,128)} reshape(f32[12,96,8,64]{1,0,3,2:T(8,128)} %copy.65) | data formatting | bytes 4718592 | tf_op jit(solution)/shard_map/convert_element_type | solution.py:75
  245.6 7.2 %fusion.13 = bf16[1152,512]{1,0:T(8,128)(2,1)} fusion(bf16[1024,512]{1,0:T(8,128)(2,1)} %param.26, bf16[1152,512]{1,0:T(8,128)(2,1)} %bitcast.178, f32[512]{0:T(512)} %param.27, bf16[512,1024]{1,0:T(8,128)(2,1)} %param.24, f32[1024]{0:T(1024)} %param.25, f32[1152,512]{0,1:T(8,128)} %reshape.185, f32[512]{0:T(512)} %param.23, f32[1152]{0:T(1024)S(1)} %rsqrt.12, ...), kind=kOutput, calls=%fused_computation.17 | convolution fusion | flops 2432434176 | bytes 6833152 | tf_op jit(solution)/shard_map/dot_general | solution.py:81
  (156 shorter events, 45.6 us)
Async XLA Ops:
  0.6 114.1 %copy-start = (bf16[12,384,384]{2,1,0:T(8,128)(2,1)S(1)}, bf16[12,384,384]{2,1,0:T(8,128)(2,1)}, u32[]{:S(2)}) copy-start(bf16[12,384,384]{2,1,0:T(8,128)(2,1)} %param.16) | copy-start | bytes 10616836
  5.1 32.1 %all-to-all-start = ((bf16[12,96,512]{1,0,2:T(8,128)(2,1)}), bf16[12,96,512]{1,0,2:T(8,128)(2,1)}, u32[]{:S(2)}, u32[]{:S(2)}) async-start(bf16[12,96,512]{1,0,2:T(8,128)(2,1)} %copy.53), calls=%async_computation | async-start | bytes 4194304 | tf_op jit(solution)/shard_map/all_to_all | solution.py:112
  63.2 17.1 %copy-start.48 = (f32[12,12]{1,0:T(8,128)S(1)}, f32[12,12]{1,0:T(8,128)}, u32[]{:S(2)}) copy-start(f32[12,12]{1,0:T(8,128)} %param.21) | copy-start | bytes 1732
  63.2 17.1 %copy-start.49 = (s32[12,12]{1,0:T(8,128)S(1)}, s32[12,12]{1,0:T(8,128)}, u32[]{:S(2)}) copy-start(s32[12,12]{1,0:T(8,128)} %param.19) | copy-start | bytes 1732
  63.2 41.6 %all-to-all-start.1 = ((bf16[32,2,9216]{2,1,0:T(2,128)(2,1)}), bf16[32,2,9216]{2,1,0:T(2,128)(2,1)}, u32[]{:S(2)}, u32[]{:S(2)}) async-start(bf16[32,2,9216]{2,1,0:T(2,128)(2,1)} %reshape.197), calls=%async_computation.1 | async-start | bytes 2359296 | tf_op jit(solution)/shard_map/all_to_all | solution.py:124
  126.6 7.3 %copy-start.44 = (f32[12,1,64]{2,1,0:T(1,128)S(1)}, f32[12,1,64]{2,1,0:T(1,128)}, u32[]{:S(2)}) copy-start(f32[12,1,64]{2,1,0:T(1,128)} %get-tuple-element.23) | copy-start | bytes 9220
  126.6 7.3 %copy-start.45 = (f32[12,1,64]{2,1,0:T(1,128)S(1)}, f32[12,1,64]{2,1,0:T(1,128)}, u32[]{:S(2)}) copy-start(f32[12,1,64]{2,1,0:T(1,128)} %get-tuple-element.24) | copy-start | bytes 9220
  126.6 7.9 %copy-start.42 = (f32[12,1,64]{2,1,0:T(1,128)S(1)}, f32[12,1,64]{2,1,0:T(1,128)}, u32[]{:S(2)}) copy-start(f32[12,1,64]{2,1,0:T(1,128)} %get-tuple-element.25) | copy-start | bytes 9220
  126.6 7.9 %copy-start.43 = (f32[12,1,64]{2,1,0:T(1,128)S(1)}, f32[12,1,64]{2,1,0:T(1,128)}, u32[]{:S(2)}) copy-start(f32[12,1,64]{2,1,0:T(1,128)} %get-tuple-element.26) | copy-start | bytes 9220
  126.6 8.5 %copy-start.40 = (f32[12,1,64]{2,1,0:T(1,128)S(1)}, f32[12,1,64]{2,1,0:T(1,128)}, u32[]{:S(2)}) copy-start(f32[12,1,64]{2,1,0:T(1,128)} %get-tuple-element.27) | copy-start | bytes 9220
  126.6 8.5 %copy-start.41 = (f32[12,1,64]{2,1,0:T(1,128)S(1)}, f32[12,1,64]{2,1,0:T(1,128)}, u32[]{:S(2)}) copy-start(f32[12,1,64]{2,1,0:T(1,128)} %get-tuple-element.28) | copy-start | bytes 9220
  126.6 9.1 %copy-start.38 = (f32[12,1,64]{2,1,0:T(1,128)S(1)}, f32[12,1,64]{2,1,0:T(1,128)}, u32[]{:S(2)}) copy-start(f32[12,1,64]{2,1,0:T(1,128)} %get-tuple-element.29) | copy-start | bytes 9220
  126.6 9.1 %copy-start.39 = (f32[12,1,64]{2,1,0:T(1,128)S(1)}, f32[12,1,64]{2,1,0:T(1,128)}, u32[]{:S(2)}) copy-start(f32[12,1,64]{2,1,0:T(1,128)} %get-tuple-element.30) | copy-start | bytes 9220
  126.6 9.7 %copy-start.36 = (f32[12,1,64]{2,1,0:T(1,128)S(1)}, f32[12,1,64]{2,1,0:T(1,128)}, u32[]{:S(2)}) copy-start(f32[12,1,64]{2,1,0:T(1,128)} %get-tuple-element.31) | copy-start | bytes 9220
  126.7 9.7 %copy-start.37 = (f32[12,1,64]{2,1,0:T(1,128)S(1)}, f32[12,1,64]{2,1,0:T(1,128)}, u32[]{:S(2)}) copy-start(f32[12,1,64]{2,1,0:T(1,128)} %get-tuple-element.32) | copy-start | bytes 9220
  126.7 10.3 %copy-start.34 = (f32[12,1,64]{2,1,0:T(1,128)S(1)}, f32[12,1,64]{2,1,0:T(1,128)}, u32[]{:S(2)}) copy-start(f32[12,1,64]{2,1,0:T(1,128)} %get-tuple-element.33) | copy-start | bytes 9220
  126.7 10.3 %copy-start.35 = (f32[12,1,64]{2,1,0:T(1,128)S(1)}, f32[12,1,64]{2,1,0:T(1,128)}, u32[]{:S(2)}) copy-start(f32[12,1,64]{2,1,0:T(1,128)} %get-tuple-element.34) | copy-start | bytes 9220
  126.7 13.9 %copy-start.46 = (f32[384]{0:T(512)S(1)}, f32[384]{0:T(512)}, u32[]{:S(2)}) copy-start(f32[384]{0:T(512)} %select_multiply_fusion) | copy-start | bytes 4612
  126.7 13.9 %copy-start.47 = (f32[384]{0:T(512)S(1)}, f32[384]{0:T(512)}, u32[]{:S(2)}) copy-start(f32[384]{0:T(512)} %fusion.90) | copy-start | bytes 4612
  126.7 36.8 %all-to-all-start.2 = ((bf16[32,2,9216]{2,1,0:T(2,128)(2,1)}), bf16[32,2,9216]{2,1,0:T(2,128)(2,1)S(1)}, u32[]{:S(2)}, u32[]{:S(2)}) async-start(bf16[32,2,9216]{2,1,0:T(2,128)(2,1)} %reshape.199), calls=%async_computation.2 | async-start | bytes 2359296 | tf_op jit(solution)/shard_map/all_to_all | solution.py:142
  176.3 9.6 %copy-start.32 = (f32[12,1,64]{2,1,0:T(1,128)S(1)}, f32[12,1,64]{2,1,0:T(1,128)}, u32[]{:S(2)}) copy-start(f32[12,1,64]{2,1,0:T(1,128)} %get-tuple-element.35) | copy-start | bytes 9220
  176.3 9.6 %copy-start.33 = (f32[12,1,64]{2,1,0:T(1,128)S(1)}, f32[12,1,64]{2,1,0:T(1,128)}, u32[]{:S(2)}) copy-start(f32[12,1,64]{2,1,0:T(1,128)} %get-tuple-element.40) | copy-start | bytes 9220
  176.7 11.0 %collective-permute-start = (bf16[2,772,64]{1,2,0:T(8,128)(2,1)S(1)}, bf16[2,772,64]{1,2,0:T(8,128)(2,1)S(1)}, u32[]{:S(2)}, u32[]{:S(2)}) collective-permute-start(bf16[2,772,64]{1,2,0:T(8,128)(2,1)S(1)} %get-tuple-element.12), channel_id=1, source_target_pairs={{0,8},{8,16},{16,24},{24,32},{32,40},{40,48},{48,56},{56,64},{64,7... | collective-permute-start | bytes 592904 | tf_op jit(solution)/shard_map/ppermute | solution.py:23
  178.6 10.8 %collective-permute-start.1 = (bf16[2,772,64]{1,2,0:T(8,128)(2,1)S(1)}, bf16[2,772,64]{1,2,0:T(8,128)(2,1)S(1)}, u32[]{:S(2)}, u32[]{:S(2)}) collective-permute-start(bf16[2,772,64]{1,2,0:T(8,128)(2,1)S(1)} %get-tuple-element.13), channel_id=1, source_target_pairs={{8,0},{16,8},{24,16},{32,24},{40,32},{48,40},{56,48},{64,56},{72,6... | collective-permute-start | bytes 592904 | tf_op jit(solution)/shard_map/ppermute | solution.py:26
  (32 other events, 152.6 us)
